TPU v7x, 32 devices: a whole 2x2x4 slice. The times are simulated.
32 devices in a mesh: seq: 8 (over y, x, core), head: 4 (over z).
Axes of the slice: x: 2, y: 2, z: 4, core: 2. Of those that a mesh axis runs over, the one named last changes fastest.
Arguments:
- query: bfloat16 [2, 1024, 4096], P(None, 'seq', 'head'), may hold values from -5 to 5
- keys: bfloat16 [2, 1024, 1024], P(None, 'seq', 'head'), may hold values from -5 to 5
- values: bfloat16 [2, 1024, 1024], P(None, 'seq', 'head'), may hold values from -12 to 12
- norm_gain: float32 [4096], P('head'), may hold values from 0.25 to 1.75
- in_b: bfloat16 [2048, 128], P('seq'), may hold values from -0.25 to 0.25
- out_c: bfloat16 [2048, 128], P('seq'), may hold values from -0.25 to 0.25
- step: float32 [64, 2048], P('head', 'seq'), may hold values from 0.2 to 1
- log_decay: float32 [64, 2048], P('head', 'seq'), may hold values from -2 to 0
- skip: float32 [64], P('head'), may hold values from 0.5 to 1.5
Outputs:
- mixed: bfloat16 [2048, 4096], P('seq', 'head')
All inputs are finite; a program needn't handle non-finite values.
Results may differ from a plain program's by a relative error of at most 0.012.
Values may be sent and summed in bfloat16 or wider, within the bound.
A program may use at most 128 MiB of HBM per device.

v0:
```python
import math

import jax
import jax.numpy as jnp
from jax import lax
from jax.sharding import PartitionSpec as P

HEADS = 32
HDIM = 128
SDIM = 64
STATE = 128
SPAN = 256


def from_behind(block, axis, distance):
    devices = range(lax.axis_size(axis))
    route = [((i - distance) % len(devices), i) for i in devices]
    return lax.ppermute(block, axis, route)


def partner(block, axis, stride):
    count = lax.axis_size(axis)
    route = []
    for low in range(count):
        high = low | 1 << stride
        if high != low and high < count:
            route += [(low, high), (high, low)]
    return lax.ppermute(block, axis, route)


def entering_2(value, axis, join, neutral):
    place = lax.axis_index(axis)
    gathered = jax.tree.map(
        lambda a, kind: lax.all_gather(a.astype(kind), axis), value, (jnp.bfloat16, jnp.bfloat16)
    )
    state = jax.tree.map(lambda a, e: jnp.zeros_like(a) + jnp.asarray(e, a.dtype), value, neutral)

    def one(turn, state):
        return join(
            state,
            jax.tree.map(
                lambda a, own: lax.dynamic_index_in_dim(a, turn, 0, False).astype(own.dtype),
                gathered,
                value,
            ),
        )

    return lax.fori_loop(0, place, one, state)


def combine_states(earlier, later):
    return (earlier[0] + later[0], jnp.exp(later[0])[:, None, None] * earlier[1] + later[1])


def body(query, keys, values, norm_gain, in_b, out_c, step, log_decay, skip):
    seq_count = lax.axis_size("seq")
    seq_index = lax.axis_index("seq")
    blk_rows = query.shape[1]
    feat_local = query.shape[2]
    kv_local = keys.shape[2] // HDIM
    group_size = feat_local // HDIM // kv_local
    score_scale = 1.0 / math.sqrt(HDIM)
    near_kv = from_behind((keys, values), "seq", 1)
    far_kv = from_behind((near_kv[0], near_kv[1]), "seq", 1)
    near_kv = tuple((jnp.where(seq_index == 0, member[::-1], member) for member in near_kv))
    far_kv = tuple((jnp.where(seq_index < 2, member[::-1], member) for member in far_kv))
    outputs = []
    for slot_id in range(2):
        block_id = seq_index + seq_count * slot_id
        key_rows = jnp.concatenate([far_kv[0][slot_id], near_kv[0][slot_id], keys[slot_id]], 0)
        val_rows = jnp.concatenate([far_kv[1][slot_id], near_kv[1][slot_id], values[slot_id]], 0)
        query_heads = query[slot_id].reshape(blk_rows, kv_local, group_size, HDIM)
        key_heads = key_rows.reshape(3 * blk_rows, kv_local, HDIM)
        val_heads = val_rows.reshape(3 * blk_rows, kv_local, HDIM)
        scores = (
            jnp.einsum("qgjd,kgd->gjqk", query_heads, key_heads, preferred_element_type=jnp.float32)
            * score_scale
        )
        query_pos = block_id * blk_rows + jnp.arange(blk_rows, dtype=jnp.int32)
        key_pos = (block_id - 2) * blk_rows + jnp.arange(3 * blk_rows, dtype=jnp.int32)
        window = 2 * blk_rows
        allowed = (
            (key_pos[None, :] <= query_pos[:, None])
            & (key_pos[None, :] > query_pos[:, None] - window)
            & (key_pos[None, :] >= 0)
        )
        scores = jnp.where(allowed, scores, -jnp.inf)
        row_peak = jnp.max(scores, axis=-1, keepdims=True)
        exp_terms = jnp.exp(scores - row_peak)
        row_total = jnp.sum(exp_terms, axis=-1)
        weights = exp_terms.astype(jnp.bfloat16)
        result = jnp.einsum(
            "gjqk,kgd->qgjd", weights, val_heads, preferred_element_type=jnp.float32
        )
        result = result / jnp.transpose(row_total, (2, 0, 1))[..., None]
        outputs.append(result.reshape(blk_rows, feat_local).astype(jnp.bfloat16))
    lead_slot = outputs[0]
    tail_slot = outputs[1]
    for bit_pos in reversed(range(seq_count.bit_length() - 1)):
        upper_half = jnp.right_shift(seq_index, bit_pos) % 2 == 1
        outgoing = jnp.where(upper_half, lead_slot, tail_slot)
        incoming = partner(outgoing, "seq", bit_pos)
        lead_slot = jnp.where(upper_half, incoming, lead_slot)
        tail_slot = jnp.where(upper_half, tail_slot, incoming)
    attended = jnp.concatenate([lead_slot, tail_slot], 0)
    widened = attended.astype(jnp.float32)
    row_sums = lax.psum(jnp.sum(widened * widened, axis=-1), "head")
    meansq = row_sums / (HEADS * HDIM)
    normed = (widened * norm_gain[None, :] * lax.rsqrt(meansq + 1e-06)[:, None]).astype(
        jnp.bfloat16
    )
    highest = lax.Precision.HIGHEST
    tok_rows = normed.shape[0]
    heads_ssm = step.shape[0]
    span_count = tok_rows // SPAN
    inputs_low = normed.reshape(span_count, SPAN, heads_ssm, SDIM)
    inputs = inputs_low.astype(jnp.float32)
    in_low = in_b.reshape(span_count, SPAN, STATE)
    out_low = out_c.reshape(span_count, SPAN, STATE)
    in_rows = in_low.astype(jnp.float32)
    out_rows = out_low.astype(jnp.float32)
    step_rows = step.reshape(heads_ssm, span_count, SPAN).transpose(1, 0, 2)
    decay_rows = log_decay.reshape(heads_ssm, span_count, SPAN).transpose(1, 0, 2)
    cum_log = jnp.cumsum(decay_rows, axis=2)
    causal = jnp.arange(SPAN)[:, None] >= jnp.arange(SPAN)[None, :]
    decay_mat = jnp.exp(
        jnp.where(causal[None, None], cum_log[:, :, :, None] - cum_log[:, :, None, :], -jnp.inf)
    )
    cross_terms = jnp.einsum("ctn,cun->ctu", out_low, in_low, preferred_element_type=jnp.float32)
    mixing = (decay_mat * cross_terms[:, None] * step_rows[:, :, None, :]).astype(jnp.bfloat16)
    local_out = jnp.einsum(
        "chtu,cuhe->cthe", mixing, inputs_low, preferred_element_type=jnp.float32
    )
    span_totals = cum_log[:, :, -1]
    end_weights = jnp.exp(span_totals[:, :, None] - cum_log) * step_rows
    weighted = end_weights.transpose(0, 2, 1)[..., None] * inputs
    span_states = jnp.einsum("cuhe,cun->chen", weighted, in_rows, precision=highest)
    incl_log = jnp.cumsum(span_totals, axis=0)
    excl_log = incl_log - span_totals
    dev_total = incl_log[-1]
    dev_state = jnp.einsum(
        "ch,chen->hen", jnp.exp(dev_total[None, :] - incl_log), span_states, precision=highest
    )
    earlier_mask = jnp.arange(span_count)[:, None] > jnp.arange(span_count)[None, :]
    pair_weights = jnp.exp(
        jnp.where(earlier_mask[:, :, None], excl_log[:, None, :] - incl_log[None, :, :], -jnp.inf)
    )
    local_start = jnp.einsum("kjh,jhen->khen", pair_weights, span_states, precision=highest)
    entry_scale = jnp.exp(cum_log).transpose(0, 2, 1)[..., None]
    identity = (
        jnp.zeros((heads_ssm,), jnp.float32),
        jnp.zeros((heads_ssm, SDIM, STATE), jnp.float32),
    )
    entry_term = (
        jnp.einsum("ctn,chen->cthe", out_rows, local_start, precision=highest) * entry_scale
    )
    partial_value = local_out + entry_term
    entering = entering_2((dev_total, dev_state), "seq", combine_states, identity)[1]
    correction = jnp.einsum("ctn,hen->cthe", out_rows, entering, precision=highest)
    offset_scale = jnp.exp(excl_log[:, None, :] + cum_log.transpose(0, 2, 1))[..., None]
    result = partial_value + correction * offset_scale
    result = result + skip[None, None, :, None] * inputs
    return result.reshape(tok_rows, heads_ssm * SDIM).astype(jnp.bfloat16)


def solution(mesh):
    placed = (
        P(None, "seq", "head"),
        P(None, "seq", "head"),
        P(None, "seq", "head"),
        P("head"),
        P("seq", None),
        P("seq", None),
        P("head", "seq"),
        P("head", "seq"),
        P("head"),
    )
    return jax.shard_map(
        body, mesh=mesh, in_specs=placed, out_specs=P("seq", "head"), check_vma=False
    )
```

profile of v0, /device:TPU:7, one launch (start us, length us, event | category | flops | bytes accessed | tf_op | source)
XLA Modules:
  0.0 94.2 jit_solution(1609227975789895635)
XLA Ops:
  6.5 1.1 %copy.121 = bf16[2,128,256]{1,2,0:T(8,128)(2,1)S(1)} copy(bf16[2,128,256]{2,1,0:T(8,128)(2,1)} %param.12) | data formatting | bytes 262144 | tf_op args[1]
  7.7 1.0 %copy.119 = bf16[2,128,256]{1,2,0:T(8,128)(2,1)S(1)} copy(bf16[2,128,256]{2,1,0:T(8,128)(2,1)} %param.13) | data formatting | bytes 262144 | tf_op args[2]
  8.8 0.9 fusion.66
  11.4 2.4 %collective-permute-start.3 = (bf16[2,128,256]{1,2,0:T(8,128)(2,1)S(1)}, bf16[2,128,256]{1,2,0:T(8,128)(2,1)S(1)}, u32[]{:S(2)}, u32[]{:S(2)}) collective-permute-start(bf16[2,128,256]{1,2,0:T(8,128)(2,1)S(1)} %collective-permute-done.2), channel_id=1, source_target_pairs={{28,0},{0,4},{4,8},{8,12},{12,16},{16,20},{20,24},{24,28},{29,1},{... | collective-permute-start | bytes 393224 | tf_op jit(solution)/shard_map/ppermute | solution.py:18
  13.8 0.6 collective-permute-start.1
  14.4 1.3 %collective-permute-done.3 = bf16[2,128,256]{1,2,0:T(8,128)(2,1)S(1)} collective-permute-done((bf16[2,128,256]{1,2,0:T(8,128)(2,1)S(1)}, bf16[2,128,256]{1,2,0:T(8,128)(2,1)S(1)}, u32[]{:S(2)}, u32[]{:S(2)}) %collective-permute-start.3) | collective-permute-done | bytes 131104 | tf_op jit(solution)/shard_map/ppermute | solution.py:18
  15.7 1.4 %collective-permute-done.1 = bf16[2,128,256]{1,2,0:T(8,128)(2,1)S(1)} collective-permute-done((bf16[2,128,256]{1,2,0:T(8,128)(2,1)S(1)}, bf16[2,128,256]{1,2,0:T(8,128)(2,1)S(1)}, u32[]{:S(2)}, u32[]{:S(2)}) %collective-permute-start.1) | collective-permute-done | bytes 131104 | tf_op jit(solution)/shard_map/ppermute | solution.py:18
  17.4 0.4 fusion.71
  18.6 0.4 fusion.22
  19.1 0.4 fusion.23
  19.6 1.6 %collective-permute-start.4 = (bf16[128,1024]{0,1:T(8,128)(2,1)S(1)}, bf16[128,1024]{0,1:T(8,128)(2,1)S(1)}, u32[]{:S(2)}, u32[]{:S(2)}) collective-permute-start(bf16[128,1024]{0,1:T(8,128)(2,1)S(1)} %bitcast_select_fusion.3), channel_id=1, source_target_pairs={{0,16},{16,0},{4,20},{20,4},{8,24},{24,8},{12,28},{28,12},{1,17},{... | collective-permute-start | bytes 786440 | tf_op jit(solution)/shard_map/ppermute | solution.py:28
  21.2 0.6 reduce-window.6
  22.0 3.9 %collective-permute-done.4 = bf16[128,1024]{0,1:T(8,128)(2,1)S(1)} collective-permute-done((bf16[128,1024]{0,1:T(8,128)(2,1)S(1)}, bf16[128,1024]{0,1:T(8,128)(2,1)S(1)}, u32[]{:S(2)}, u32[]{:S(2)}) %collective-permute-start.4) | collective-permute-done | bytes 262176 | tf_op jit(solution)/shard_map/ppermute | solution.py:28
  26.3 5.0 %collective-permute-done.5 = bf16[128,1024]{0,1:T(8,128)(2,1)S(1)} collective-permute-done((bf16[128,1024]{0,1:T(8,128)(2,1)S(1)}, bf16[128,1024]{0,1:T(8,128)(2,1)S(1)}, u32[]{:S(2)}, u32[]{:S(2)}) %collective-permute-start.5) | collective-permute-done | bytes 262176 | tf_op jit(solution)/shard_map/ppermute | solution.py:28
  31.3 3.8 %collective-permute-start.6 = (bf16[128,1024]{0,1:T(8,128)(2,1)S(1)}, bf16[128,1024]{0,1:T(8,128)(2,1)S(1)}, u32[]{:S(2)}, u32[]{:S(2)}) collective-permute-start(bf16[128,1024]{0,1:T(8,128)(2,1)S(1)} %broadcast_select_fusion.5), channel_id=1, source_target_pairs={{0,4},{4,0},{8,12},{12,8},{16,20},{20,16},{24,28},{28,24},{1,5},{5... | collective-permute-start | bytes 786440 | tf_op jit(solution)/shard_map/ppermute | solution.py:28
  35.4 0.9 collective-permute-done.6
  36.5 10.2 %psum.7 = f32[256]{0:T(256)S(1)} all-reduce(f32[256]{0:T(256)S(1)} %multiply_reduce_fusion), channel_id=1, replica_groups=mesh['seq'=8,'head'=4] {'head'}, use_global_device_ids=true, to_apply=%region_5.6 | all-reduce | flops 256 | bytes 2048 | tf_op jit(solution)/shard_map/psum | solution.py:107
  46.7 1.5 %multiply_convert_fusion.14 = (bf16[16,64,128]{2,1,0:T(8,128)(2,1)}, f32[16,64,128]{2,1,0:T(8,128)S(1)}) fusion(f32[16]{0:T(128)S(1)} %get-tuple-element.72, bf16[256,128]{1,0:T(8,128)(2,1)S(1)} %copy-done.2, f32[256,16]{0,1:T(8,128)S(1)} %get-tuple-element.65, f32[256]{0:T(256)S(1)} %add_rsqrt_fusion, f32[16,64]{1,0:T(8,128)S(1)} %mul.192, ...), kind=kOutput, calls=%fused_computation.43 | convolution fusion | flops 405274624 | bytes 1397824 | tf_op jit(solution)/shard_map/cuhe,cun->chen/dot_general | solution.py:137
  48.2 11.5 %all-gather = bf16[8,16,1]{1,2,0:T(2,128)(2,1)S(1)} all-gather(bf16[1,16,1]{1,2,0:T(2,128)(2,1)S(1)} %slice.88), channel_id=2, replica_groups=mesh['seq'=8,'head'=4] {'seq'}, dimensions={0}, use_global_device_ids=true | all-gather | bytes 288 | tf_op jit(solution)/shard_map/all_gather | solution.py:34
  60.1 0.6 fusion.13
  60.7 15.3 %all-gather.4.cloned.1.call-done = bf16[128,64,128]{2,1,0:T(8,128)(2,1)} async-done(((bf16[16,64,128]{2,1,0:T(8,128)(2,1)}), bf16[128,64,128]{2,1,0:T(8,128)(2,1)}) %all-gather.4.cloned.1.call-update) | async-done | bytes 2097168 | tf_op jit(solution)/shard_map/all_gather | solution.py:34
  76.0 8.1 %while.12 = (s32[]{:T(128)}, f32[16,64,128]{2,1,0:T(8,128)S(1)}, s32[]{:T(128)}, bf16[8,16]{1,0:T(8,128)(2,1)S(1)}, bf16[8,16,64,128]{3,2,1,0:T(8,128)(2,1)}, /*index=5*/s32[]{:T(128)}, s32[]{:T(128)}, s32[]{:T(128)}) while((s32[]{:T(128)}, f32[16,64,128]{2,1,0:T(8,128)S(1)}, s32[]{:T(128)}, bf16[8,16]{1,0:T(8,128)(2,1)S(1)}, ...), condition=%wide.region_9.10_spmd, body=%wide.region_8.9_spmd.sunk | while | flops 393237 | bytes 1311007 | solution.py:48
  76.0 1.1 %convert_add_fusion.2 = f32[16,64,128]{2,1,0:T(8,128)S(1)} fusion(f32[16,64,128]{2,1,0:T(8,128)S(1)} %get-tuple-element.138, bf16[8,16,64,128]{3,2,1,0:T(8,128)(2,1)} %get-tuple-element.149, s32[]{:T(128)S(6)} %select_n.192, f32[16]{0:T(128)S(1)} %exponential_bitcast_fusion.4), kind=kLoop, calls=%fused_computation.clone.1 | loop fusion | flops 393216 | bytes 1310788 | tf_op jit(solution)/shard_map/while/body/add | solution.py:52
  77.2 1.1 %convert_add_fusion.2 = f32[16,64,128]{2,1,0:T(8,128)S(1)} fusion(f32[16,64,128]{2,1,0:T(8,128)S(1)} %get-tuple-element.138, bf16[8,16,64,128]{3,2,1,0:T(8,128)(2,1)} %get-tuple-element.149, s32[]{:T(128)S(6)} %select_n.192, f32[16]{0:T(128)S(1)} %exponential_bitcast_fusion.4), kind=kLoop, calls=%fused_computation.clone.1 | loop fusion | flops 393216 | bytes 1310788 | tf_op jit(solution)/shard_map/while/body/add | solution.py:52
  78.4 1.1 %convert_add_fusion.2 = f32[16,64,128]{2,1,0:T(8,128)S(1)} fusion(f32[16,64,128]{2,1,0:T(8,128)S(1)} %get-tuple-element.138, bf16[8,16,64,128]{3,2,1,0:T(8,128)(2,1)} %get-tuple-element.149, s32[]{:T(128)S(6)} %select_n.192, f32[16]{0:T(128)S(1)} %exponential_bitcast_fusion.4), kind=kLoop, calls=%fused_computation.clone.1 | loop fusion | flops 393216 | bytes 1310788 | tf_op jit(solution)/shard_map/while/body/add | solution.py:52
  79.5 1.1 %convert_add_fusion.2 = f32[16,64,128]{2,1,0:T(8,128)S(1)} fusion(f32[16,64,128]{2,1,0:T(8,128)S(1)} %get-tuple-element.138, bf16[8,16,64,128]{3,2,1,0:T(8,128)(2,1)} %get-tuple-element.149, s32[]{:T(128)S(6)} %select_n.192, f32[16]{0:T(128)S(1)} %exponential_bitcast_fusion.4), kind=kLoop, calls=%fused_computation.clone.1 | loop fusion | flops 393216 | bytes 1310788 | tf_op jit(solution)/shard_map/while/body/add | solution.py:52
  80.7 1.1 %convert_add_fusion.2 = f32[16,64,128]{2,1,0:T(8,128)S(1)} fusion(f32[16,64,128]{2,1,0:T(8,128)S(1)} %get-tuple-element.138, bf16[8,16,64,128]{3,2,1,0:T(8,128)(2,1)} %get-tuple-element.149, s32[]{:T(128)S(6)} %select_n.192, f32[16]{0:T(128)S(1)} %exponential_bitcast_fusion.4), kind=kLoop, calls=%fused_computation.clone.1 | loop fusion | flops 393216 | bytes 1310788 | tf_op jit(solution)/shard_map/while/body/add | solution.py:52
  81.8 1.1 %convert_add_fusion.2 = f32[16,64,128]{2,1,0:T(8,128)S(1)} fusion(f32[16,64,128]{2,1,0:T(8,128)S(1)} %get-tuple-element.138, bf16[8,16,64,128]{3,2,1,0:T(8,128)(2,1)} %get-tuple-element.149, s32[]{:T(128)S(6)} %select_n.192, f32[16]{0:T(128)S(1)} %exponential_bitcast_fusion.4), kind=kLoop, calls=%fused_computation.clone.1 | loop fusion | flops 393216 | bytes 1310788 | tf_op jit(solution)/shard_map/while/body/add | solution.py:52
  83.0 1.1 %convert_add_fusion.2 = f32[16,64,128]{2,1,0:T(8,128)S(1)} fusion(f32[16,64,128]{2,1,0:T(8,128)S(1)} %get-tuple-element.138, bf16[8,16,64,128]{3,2,1,0:T(8,128)(2,1)} %get-tuple-element.149, s32[]{:T(128)S(6)} %select_n.192, f32[16]{0:T(128)S(1)} %exponential_bitcast_fusion.4), kind=kLoop, calls=%fused_computation.clone.1 | loop fusion | flops 393216 | bytes 1310788 | tf_op jit(solution)/shard_map/while/body/add | solution.py:52
  84.1 0.6 fusion.15
  84.8 1.6 %fusion.19 = bf16[1,256,16,64]{1,3,2,0:T(8,128)(2,1)S(1)} fusion(f32[1,256,16,64]{1,3,2,0:T(8,128)S(1)} %fusion.15, f32[1,256,16,64]{1,3,2,0:T(8,128)S(1)} %fusion.13, f32[16,256]{1,0:T(8,128)S(1)} %copy-done.3, f32[256,256]{1,0:T(8,128)S(1)} %fusion.72, f32[16,256]{1,0:T(8,128)S(1)} %get-tuple-element.66, pred[256,256]{1,0:T(8,128)(4,1)S(1)} %iota_compare_fusion, ...), kind=kOutput, calls=%fused_computation.28 | convolution fusion | flops 144703488 | bytes 4035648 | tf_op jit(solution)/shard_map/chtu,cuhe->cthe/dot_general | solution.py:131
  86.4 1.0 %copy.144 = bf16[256,1024]{1,0:T(8,128)(2,1)} copy(bf16[256,1024]{0,1:T(8,128)(2,1)S(1)} %bitcast.165) | data formatting | bytes 1048576 | tf_op jit(solution)/shard_map/convert_element_type | solution.py:163
  (87 shorter events, 4.5 us)
Async XLA Ops:
  6.5 53.3 %copy-start = (bf16[256,128]{1,0:T(8,128)(2,1)S(1)}, bf16[256,128]{1,0:T(8,128)(2,1)}, u32[]{:S(2)}) copy-start(bf16[256,128]{1,0:T(8,128)(2,1)} %param.16) | copy-start | bytes 196612
  6.5 3.4 %copy-start.1 = (bf16[2,128,1024]{2,1,0:T(8,128)(2,1)S(1)}, bf16[2,128,1024]{2,1,0:T(8,128)(2,1)}, u32[]{:S(2)}) copy-start(bf16[2,128,1024]{2,1,0:T(8,128)(2,1)} %param.11) | copy-start | bytes 1572868
  6.5 69.4 %all-gather.4.cloned.1.call-start = ((), (), s32[]{:S(2)}) async-start(), calls=%async_computation | async-start | bytes 2359296 | tf_op jit(solution)/shard_map/all_gather | solution.py:34
  7.6 3.4 %collective-permute-start.2 = (bf16[2,128,256]{1,2,0:T(8,128)(2,1)S(1)}, bf16[2,128,256]{1,2,0:T(8,128)(2,1)S(1)}, u32[]{:S(2)}, u32[]{:S(2)}) collective-permute-start(bf16[2,128,256]{1,2,0:T(8,128)(2,1)S(1)} %copy.121), channel_id=1, source_target_pairs={{28,0},{0,4},{4,8},{8,12},{12,16},{16,20},{20,24},{24,28},{29,1},{... | collective-permute-start | bytes 393224 | tf_op jit(solution)/shard_map/ppermute | solution.py:18
  8.7 5.0 %collective-permute-start = (bf16[2,128,256]{1,2,0:T(8,128)(2,1)S(1)}, bf16[2,128,256]{1,2,0:T(8,128)(2,1)S(1)}, u32[]{:S(2)}, u32[]{:S(2)}) collective-permute-start(bf16[2,128,256]{1,2,0:T(8,128)(2,1)S(1)} %copy.119), channel_id=1, source_target_pairs={{28,0},{0,4},{4,8},{8,12},{12,16},{16,20},{20,24},{24,28},{29,1},{... | collective-permute-start | bytes 393224 | tf_op jit(solution)/shard_map/ppermute | solution.py:18
  11.4 4.3 %collective-permute-start.3 = (bf16[2,128,256]{1,2,0:T(8,128)(2,1)S(1)}, bf16[2,128,256]{1,2,0:T(8,128)(2,1)S(1)}, u32[]{:S(2)}, u32[]{:S(2)}) collective-permute-start(bf16[2,128,256]{1,2,0:T(8,128)(2,1)S(1)} %collective-permute-done.2), channel_id=1, source_target_pairs={{28,0},{0,4},{4,8},{8,12},{12,16},{16,20},{20,24},{24,28},{29,1},{... | collective-permute-start | bytes 393224 | tf_op jit(solution)/shard_map/ppermute | solution.py:18
  13.8 3.3 %collective-permute-start.1 = (bf16[2,128,256]{1,2,0:T(8,128)(2,1)S(1)}, bf16[2,128,256]{1,2,0:T(8,128)(2,1)S(1)}, u32[]{:S(2)}, u32[]{:S(2)}) collective-permute-start(bf16[2,128,256]{1,2,0:T(8,128)(2,1)S(1)} %collective-permute-done), channel_id=1, source_target_pairs={{28,0},{0,4},{4,8},{8,12},{12,16},{16,20},{20,24},{24,28},{29,1},{... | collective-permute-start | bytes 393224 | tf_op jit(solution)/shard_map/ppermute | solution.py:18
  19.1 2.1 %copy-start.4 = (f32[16,256]{1,0:T(8,128)S(1)}, f32[16,256]{1,0:T(8,128)}, u32[]{:S(2)}) copy-start(f32[16,256]{1,0:T(8,128)} %param.18) | copy-start | bytes 49156
  19.6 6.3 %collective-permute-start.4 = (bf16[128,1024]{0,1:T(8,128)(2,1)S(1)}, bf16[128,1024]{0,1:T(8,128)(2,1)S(1)}, u32[]{:S(2)}, u32[]{:S(2)}) collective-permute-start(bf16[128,1024]{0,1:T(8,128)(2,1)S(1)} %bitcast_select_fusion.3), channel_id=1, source_target_pairs={{0,16},{16,0},{4,20},{20,4},{8,24},{24,8},{12,28},{28,12},{1,17},{... | collective-permute-start | bytes 786440 | tf_op jit(solution)/shard_map/ppermute | solution.py:28
  22.0 13.2 %copy-start.5 = (f32[1024]{0:T(1024)S(1)}, f32[1024]{0:T(1024)}, u32[]{:S(2)}) copy-start(f32[1024]{0:T(1024)} %param.14) | copy-start | bytes 12292
  22.0 13.3 %copy-start.3 = (f32[16,256]{1,0:T(8,128)S(1)}, f32[16,256]{1,0:T(8,128)}, u32[]{:S(2)}) copy-start(f32[16,256]{1,0:T(8,128)} %param.17) | copy-start | bytes 49156
  26.0 5.3 %collective-permute-start.5 = (bf16[128,1024]{0,1:T(8,128)(2,1)S(1)}, bf16[128,1024]{0,1:T(8,128)(2,1)S(1)}, u32[]{:S(2)}, u32[]{:S(2)}) collective-permute-start(bf16[128,1024]{0,1:T(8,128)(2,1)S(1)} %get-tuple-element.62), channel_id=1, source_target_pairs={{0,8},{8,0},{4,12},{12,4},{16,24},{24,16},{20,28},{28,20},{1,9},{9... | collective-permute-start | bytes 786440 | tf_op jit(solution)/shard_map/ppermute | solution.py:28
  31.3 15.4 %copy-start.2 = (bf16[256,128]{1,0:T(8,128)(2,1)S(1)}, bf16[256,128]{1,0:T(8,128)(2,1)}, u32[]{:S(2)}) copy-start(bf16[256,128]{1,0:T(8,128)(2,1)} %param.15) | copy-start | bytes 196612
  31.3 4.9 %collective-permute-start.6 = (bf16[128,1024]{0,1:T(8,128)(2,1)S(1)}, bf16[128,1024]{0,1:T(8,128)(2,1)S(1)}, u32[]{:S(2)}, u32[]{:S(2)}) collective-permute-start(bf16[128,1024]{0,1:T(8,128)(2,1)S(1)} %broadcast_select_fusion.5), channel_id=1, source_target_pairs={{0,4},{4,0},{8,12},{12,8},{16,20},{20,16},{24,28},{28,24},{1,5},{5... | collective-permute-start | bytes 786440 | tf_op jit(solution)/shard_map/ppermute | solution.py:28
  84.1 0.7 copy-start.6
Sparse Core Ops, SparseCore 0:
  48.3 27.5 all-gather.3
where the time goes:
time: 94.6 us; the launch traced here: 94.2 us
  waiting for transfers between devices  27.7 us (29%)
  blocking collectives  21.6 us (23%)
  between operations  13.9 us (15%)
  other arithmetic  10 us (11%)
  starting transfers between devices  8.6 us (9%)
  local copies, waits for them, and re-layouts  6.09 us (6%)
  matrix products  5.98 us (6%)
    all_gather x1, waiting for transfers between devices, entering_2(): lax.all_gather(a.astype(kind), axis)  15.3 us
    all_gather x1, blocking collectives, entering_2(): lax.all_gather(a.astype(kind), axis)  11.5 us
    psum x1, blocking collectives, body(): row_sums = lax.psum(jnp.sum(widened * widened, axis=-1), 'head')  10.2 us
    ppermute x3, waiting for transfers between devices, partner(): return lax.ppermute(block, axis, route)  9.79 us
    add x7, other arithmetic, combine_states(): jnp.exp(later[0])[:, None, None] * earlier[1] + later[1]  7.78 us
    ppermute x3, starting transfers between devices, partner(): return lax.ppermute(block, axis, route)  5.49 us
    ppermute x4, starting transfers between devices, from_behind(): return lax.ppermute(block, axis, route)  3.1 us
    ppermute x4, waiting for transfers between devices, from_behind(): return lax.ppermute(block, axis, route)  2.65 us
  transfers between devices with their start and end apart: 8, of which 6 were waited for; matrix products, arithmetic and copies ran while one was open for 6% of the time, Pallas kernels for 0%

commit v1 on v0

v1 whole, which is shorter than its diff:
```python
import functools
import math

import jax
import jax.numpy as jnp
from jax import lax
from jax.experimental import pallas as pl
from jax.experimental.pallas import tpu as pltpu
from jax.sharding import PartitionSpec as P

HDIM = 128
LANES = 128
F32 = jnp.float32
BF16 = jnp.bfloat16
MESH = pl.DeviceIdType.MESH


def remote(src, dst, send_sem, recv_sem, **where):
    return pltpu.make_async_remote_copy(
        src_ref=src,
        dst_ref=dst,
        send_sem=send_sem,
        recv_sem=recv_sem,
        device_id=where,
        device_id_type=MESH,
    )


def arrived(dst, sem):
    pltpu.make_async_copy(dst, dst, sem).wait()


def dot(a, b, dims, precision=None):
    return lax.dot_general(
        a, b, (dims, ((), ())), precision=precision, preferred_element_type=F32
    )


def kernel(
    n, nh,
    q_ref, k_ref, v_ref, gain_ref, b_ref, c_ref, step_ref, decay_ref, skip_ref,
    out_ref,
    q_buf, k_buf, v_buf, att, sumsq, mix, cum_buf, w_full, e_full, part,
    tot_buf, tot_own, ms_buf, ms_own, s_own, s_peer, t_chip, s_chips, p_own, p_peer,
    q_send, q_recv, kv_send, kv_recv, fwd_send,
    tot_send, tot_recv, ms_send, ms_recv, a_send, a_recv, b_send, b_recv, c_send, c_recv,
):
    me = lax.axis_index("seq")
    mz = lax.axis_index("head")
    core = lax.rem(me, 2)
    chip = me // 2
    chips = n // 2
    peer = me + 1 - 2 * core
    blk = q_ref.shape[1]
    feats = q_ref.shape[2]
    kv_local = k_ref.shape[2] // HDIM
    group = feats // HDIM // kv_local
    gcols = group * HDIM
    toks = 2 * blk
    heads = step_ref.shape[0]
    sdim = feats // heads
    tiles = feats // LANES
    half = feats // 2
    htiles = tiles // 2

    barrier = pltpu.get_barrier_semaphore()

    @pl.loop(1, n)
    def _(off):
        pl.semaphore_signal(
            barrier, inc=1, device_id={"seq": lax.rem(me + off, n)}, device_id_type=MESH
        )

    @pl.loop(1, nh)
    def _(off):
        pl.semaphore_signal(
            barrier, inc=1, device_id={"head": lax.rem(mz + off, nh)}, device_id_type=MESH
        )

    pl.semaphore_wait(barrier, n + nh - 2)

    def moves(g):
        found = []
        for s in range(2):
            home = (n // 2) * s + chip
            kcols = pl.ds(g * HDIM, HDIM)
            qcols = pl.ds(g * gcols, gcols)
            for t, (src, dst) in enumerate(((k_ref, k_buf), (v_ref, v_buf))):
                found.append((
                    src.at[s, :, kcols],
                    dst.at[pl.ds((2 + core) * blk, blk), kcols],
                    kv_send.at[g, s, 0, t], kv_recv.at[g, 2 + core, t], home, None,
                ))
                found.append((
                    src.at[s, :, kcols],
                    dst.at[pl.ds(core * blk, blk), kcols],
                    kv_send.at[g, s, 1, t], kv_recv.at[g, core, t], home + 1,
                    (lax.rem(home, 2) == 1) & (home + 1 < n),
                ))
            found.append((
                q_ref.at[s, :, qcols],
                q_buf.at[pl.ds(core * blk, blk), qcols],
                q_send.at[g, s], q_recv.at[g, core], home, None,
            ))
        return found

    def away(dest, cond):
        other = dest != me
        return other if cond is None else other & cond

    for g in range(kv_local):
        for src, dst, ssem, rsem, dest, cond in moves(g):

            @pl.when(away(dest, cond))
            def _():
                remote(src, dst, ssem, rsem, seq=dest).start()

            here = dest == me
            here = here if cond is None else here & cond

            @pl.when(here)
            def _():
                pltpu.make_async_copy(src, dst, rsem).start()

    @pl.when(me == 0)
    def _():
        k_buf[0:toks] = jnp.zeros_like(k_buf[0:toks])
        v_buf[0:toks] = jnp.zeros_like(v_buf[0:toks])

    t_ids = lax.broadcasted_iota(jnp.int32, (toks, toks), 0)
    u_ids = lax.broadcasted_iota(jnp.int32, (toks, toks), 1)
    upper = (t_ids <= u_ids).astype(F32)
    cum = dot(decay_ref[...], upper, ((1,), (0,)), lax.Precision.HIGHEST)
    cum_buf[...] = cum
    pick = (
        lax.broadcasted_iota(jnp.int32, (heads, feats), 1) // sdim
        == lax.broadcasted_iota(jnp.int32, (heads, feats), 0)
    ).astype(F32)
    total = jnp.sum(decay_ref[...], axis=1, keepdims=True)
    tot_row = jnp.sum(total * pick, axis=0, keepdims=True)
    for p in range(tiles):
        tot_own[p : p + 1, :] = tot_row[:, p * LANES : (p + 1) * LANES]

    def tot_copy(dest, source):
        return remote(
            tot_own, tot_buf.at[source], tot_send.at[dest], tot_recv.at[source], seq=dest
        )

    @pl.loop(1, n)
    def _(off):
        tot_copy(lax.rem(me + off, n), me).start()

    tot_buf[me] = tot_own[...]

    def expand(rows):
        high = rows.astype(BF16)
        low = (rows - high.astype(F32)).astype(BF16)
        both = jnp.concatenate([high, low], 0)
        pick2 = jnp.concatenate([pick, pick], 0).astype(BF16)
        return dot(both, pick2, ((0,), (0,)))

    w_full[...] = expand(jnp.exp(cum[:, toks - 1 : toks] - cum) * step_ref[...])
    e_full[...] = expand(jnp.exp(cum))
    cross = dot(c_ref[...], b_ref[...], ((1,), (1,)))
    part[:, 0:toks] = jnp.where(t_ids >= u_ids, cross, 0.0)

    @pl.loop(0, heads)
    def _(h):
        row = cum_buf[pl.ds(h, 1), :]
        col = jnp.transpose(jnp.broadcast_to(row, (LANES, toks)))
        srow = step_ref[pl.ds(h, 1), :]
        for lo in range(0, toks, LANES):
            cols = slice(lo, lo + LANES)
            diff = jnp.minimum(col - row[:, cols], 0.0)
            mix[h, :, cols] = (jnp.exp(diff) * part[:, cols] * srow[:, cols]).astype(BF16)

    factor = math.log2(math.e) / math.sqrt(HDIM)
    r_ids = lax.broadcasted_iota(jnp.int32, (blk, blk), 0)
    c_ids = lax.broadcasted_iota(jnp.int32, (blk, blk), 1)
    sumsq[...] = jnp.zeros_like(sumsq)
    for g in range(kv_local):
        kcols = slice(g * HDIM, (g + 1) * HDIM)
        for slot in (2, 3):
            for t, buf in enumerate((k_buf, v_buf)):
                arrived(
                    buf.at[pl.ds(slot * blk, blk), pl.ds(g * HDIM, HDIM)],
                    kv_recv.at[g, slot, t],
                )

        @pl.when(core == 0)
        def _():
            for slot in (2, 3):
                for t, buf in enumerate((k_buf, v_buf)):
                    remote(
                        buf.at[pl.ds(slot * blk, blk), pl.ds(g * HDIM, HDIM)],
                        buf.at[pl.ds((slot - 2) * blk, blk), pl.ds(g * HDIM, HDIM)],
                        fwd_send.at[g, slot - 2, t], kv_recv.at[g, slot - 2, t], seq=peer,
                    ).start()

        @pl.when(me > 0)
        def _():
            for slot in (0, 1):
                for t, buf in enumerate((k_buf, v_buf)):
                    arrived(
                        buf.at[pl.ds(slot * blk, blk), pl.ds(g * HDIM, HDIM)],
                        kv_recv.at[g, slot, t],
                    )

        for slot in (0, 1):
            arrived(
                q_buf.at[pl.ds(slot * blk, blk), pl.ds(g * gcols, gcols)], q_recv.at[g, slot]
            )

        @pl.loop(0, group)
        def _(j):
            hcols = pl.ds(pl.multiple_of(g * gcols + j * HDIM, HDIM), HDIM)
            for slot in (0, 1):
                rows = slice(slot * blk, (slot + 1) * blk)
                keys = slice(slot * blk, (slot + 3) * blk)
                score = dot(q_buf[rows, hcols], k_buf[keys, kcols], ((1,), (1,)))
                far = (c_ids > r_ids) & (me > 0)
                mid = None if slot else jnp.broadcast_to(me > 0, (blk, blk))
                s0 = jnp.where(far, score[:, 0:blk], -jnp.inf)
                s1 = score[:, blk : 2 * blk]
                if slot == 0:
                    s1 = jnp.where(mid, s1, -jnp.inf)
                s2 = jnp.where(c_ids <= r_ids, score[:, 2 * blk :], -jnp.inf)
                peak = jnp.max(jnp.maximum(jnp.maximum(s0, s1), s2), axis=1, keepdims=True)
                e0 = jnp.exp2((s0 - peak) * factor)
                e1 = jnp.exp2((s1 - peak) * factor)
                e2 = jnp.exp2((s2 - peak) * factor)
                weight = jnp.concatenate([e0, e1, e2], 1).astype(BF16)
                whole = jnp.sum(e0 + e1 + e2, axis=1, keepdims=True)
                result = dot(weight, v_buf[keys, kcols], ((1,), (0,))) / whole
                result = result.astype(BF16)
                att[rows, hcols] = result
                wide = result.astype(F32)
                sumsq[rows, :] += wide * wide

    ms_row = jnp.sum(jnp.transpose(sumsq[...]), axis=0, keepdims=True)
    ms_own[...] = jnp.broadcast_to(ms_row, ms_own.shape)

    def ms_copy(dest, source):
        return remote(
            ms_own, ms_buf.at[source], ms_send.at[dest], ms_recv.at[source], head=dest
        )

    @pl.loop(1, nh)
    def _(off):
        ms_copy(lax.rem(mz + off, nh), mz).start()

    ms_buf[mz] = ms_own[...]

    @pl.loop(1, nh)
    def _(off):
        arrived(ms_buf.at[lax.rem(mz + off, nh)], ms_recv.at[lax.rem(mz + off, nh)])

    meansq = jnp.sum(ms_buf[...], axis=0)[0:1, :] * (1.0 / (feats * nh))
    scale = jnp.transpose(jnp.broadcast_to(lax.rsqrt(meansq + 1e-06), (LANES, toks)))

    b_turned = jnp.transpose(b_ref[...].astype(F32)).astype(BF16)
    for p in range(tiles):
        cols = slice(p * LANES, (p + 1) * LANES)
        normed = (att[:, cols].astype(F32) * gain_ref[:, cols] * scale).astype(BF16)
        att[:, cols] = normed
        scaled = (normed.astype(F32) * w_full[:, cols]).astype(BF16)
        into = slice((p % htiles) * LANES, (p % htiles + 1) * LANES)
        s_own[p // htiles, :, into] = dot(b_turned, scaled, ((1,), (0,))).astype(BF16)

    a_copy = remote(s_own, s_peer, a_send, a_recv, seq=peer)
    a_copy.start()

    @pl.loop(1, n)
    def _(off):
        arrived(tot_buf.at[lax.rem(me + off, n)], tot_recv.at[lax.rem(me + off, n)])

    def row_of(device, side):
        return jnp.concatenate(
            [tot_buf[device, pl.ds(side * htiles + q, 1), :] for q in range(htiles)], 1
        )

    even = core == 0
    one = jnp.ones((1, half), F32)
    mine_scale = jnp.where(even, jnp.exp(row_of(peer, core)), one)
    peer_scale = jnp.where(even, one, jnp.exp(row_of(me, core)))
    a_copy.wait_recv()
    t_chip[...] = (
        mine_scale * s_own[core].astype(F32) + peer_scale * s_peer[core].astype(F32)
    ).astype(BF16)

    def b_copy(dest, source):
        return remote(
            t_chip, s_chips.at[source], b_send.at[dest], b_recv.at[source],
            seq=2 * dest + core,
        )

    @pl.loop(chip + 1, chips)
    def _(dest):
        b_copy(dest, chip).start()

    left = lax.broadcasted_iota(jnp.int32, (toks, LANES), 1) < sdim
    skip_row = jnp.sum(skip_ref[...] * pick, axis=0, keepdims=True)
    for p in range(tiles):
        cols = slice(p * LANES, (p + 1) * LANES)
        x = att[:, cols]
        zero = jnp.zeros_like(x)
        y = dot(mix[2 * p], jnp.where(left, x, zero), ((1,), (0,)))
        y += dot(mix[2 * p + 1], jnp.where(left, zero, x), ((1,), (0,)))
        part[:, cols] = y + skip_row[:, cols] * x.astype(F32)

    w_full[0 : s_own.shape[1], 0:half] = jnp.zeros((s_own.shape[1], half), F32)
    state = w_full.at[0 : s_own.shape[1], 0:half]

    @pl.loop(0, chip)
    def _(source):
        arrived(s_chips.at[source], b_recv.at[source])
        decay = jnp.exp(row_of(2 * source, core) + row_of(2 * source + 1, core))
        state[...] = decay * state[...] + s_chips[source].astype(F32)

    p_own[...] = state[...].astype(BF16)
    c_copy = remote(p_own, p_peer, c_send, c_recv, seq=peer)
    c_copy.start()

    def finish(side, entered):
        lanes = slice(side * half, (side + 1) * half)
        keep = jnp.where(even, one, jnp.exp(row_of(peer, side)))
        add = jnp.where(even, jnp.zeros_like(one), one)
        entering = keep * entered.astype(F32) + add * s_peer[side].astype(F32)
        term = dot(c_ref[...], entering.astype(BF16), ((1,), (0,)))
        out_ref[:, lanes] = (part[:, lanes] + term * e_full[:, lanes]).astype(BF16)

    c_copy.wait_recv()
    for side in range(2):
        finish(side, jnp.where(core == side, p_own[...], p_peer[...]))

    for g in range(kv_local):
        for src, dst, ssem, rsem, dest, cond in moves(g):

            @pl.when(away(dest, cond))
            def _():
                remote(src, dst, ssem, rsem, seq=dest).wait_send()

        @pl.when(core == 0)
        def _():
            for slot in (2, 3):
                for t, buf in enumerate((k_buf, v_buf)):
                    remote(
                        buf.at[pl.ds(slot * blk, blk), pl.ds(g * HDIM, HDIM)],
                        buf.at[pl.ds((slot - 2) * blk, blk), pl.ds(g * HDIM, HDIM)],
                        fwd_send.at[g, slot - 2, t], kv_recv.at[g, slot - 2, t], seq=peer,
                    ).wait_send()

    @pl.loop(1, n)
    def _(off):
        tot_copy(lax.rem(me + off, n), me).wait_send()

    @pl.loop(1, nh)
    def _(off):
        ms_copy(lax.rem(mz + off, nh), mz).wait_send()

    @pl.loop(chip + 1, chips)
    def _(dest):
        b_copy(dest, chip).wait_send()

    a_copy.wait_send()
    c_copy.wait_send()


def body(query, keys, values, norm_gain, in_b, out_c, step, log_decay, skip):
    n = lax.axis_size("seq")
    nh = lax.axis_size("head")
    blk, feats = query.shape[1], query.shape[2]
    kvcols = keys.shape[2]
    kv_local = kvcols // HDIM
    toks = 2 * blk
    heads = step.shape[0]
    nstate = in_b.shape[1]
    tiles = feats // LANES
    half = feats // 2
    chips = n // 2
    dma = pltpu.SemaphoreType.DMA
    vmem = pl.BlockSpec(memory_space=pltpu.VMEM)
    return pl.pallas_call(
        functools.partial(kernel, n, nh),
        out_shape=jax.ShapeDtypeStruct((toks, feats), BF16),
        in_specs=[vmem] * 9,
        out_specs=vmem,
        scratch_shapes=[
            pltpu.VMEM((toks, feats), BF16),
            pltpu.VMEM((2 * toks, kvcols), BF16),
            pltpu.VMEM((2 * toks, kvcols), BF16),
            pltpu.VMEM((toks, feats), BF16),
            pltpu.VMEM((toks, LANES), F32),
            pltpu.VMEM((heads, toks, toks), BF16),
            pltpu.VMEM((heads, toks), F32),
            pltpu.VMEM((toks, feats), F32),
            pltpu.VMEM((toks, feats), F32),
            pltpu.VMEM((toks, feats), F32),
            pltpu.VMEM((n, tiles, LANES), F32),
            pltpu.VMEM((tiles, LANES), F32),
            pltpu.VMEM((nh, 8, toks), F32),
            pltpu.VMEM((8, toks), F32),
            pltpu.VMEM((2, nstate, half), BF16),
            pltpu.VMEM((2, nstate, half), BF16),
            pltpu.VMEM((nstate, half), BF16),
            pltpu.VMEM((chips, nstate, half), BF16),
            pltpu.VMEM((nstate, half), BF16),
            pltpu.VMEM((nstate, half), BF16),
            dma((kv_local, 2)), dma((kv_local, 2)),
            dma((kv_local, 2, 2, 2)), dma((kv_local, 4, 2)), dma((kv_local, 2, 2)),
            dma((n,)), dma((n,)), dma((nh,)), dma((nh,)),
            dma, dma, dma((chips,)), dma((chips,)), dma, dma,
        ],
        compiler_params=pltpu.CompilerParams(
            collective_id=0, has_side_effects=True, vmem_limit_bytes=60 * 2**20
        ),
    )(
        query, keys, values, norm_gain.reshape(1, feats), in_b, out_c, step, log_decay,
        skip.reshape(heads, 1),
    )


def solution(mesh):
    placed = (
        P(None, "seq", "head"),
        P(None, "seq", "head"),
        P(None, "seq", "head"),
        P("head"),
        P("seq", None),
        P("seq", None),
        P("head", "seq"),
        P("head", "seq"),
        P("head"),
    )
    return jax.shard_map(
        body, mesh=mesh, in_specs=placed, out_specs=P("seq", "head"), check_vma=False
    )
```

time: 94.6 us -> 42 us (0.44)
  Pallas kernels: 0 us -> 38.6 us
  waiting for transfers between devices: 27.7 us -> 0 us
  blocking collectives: 21.6 us -> 0 us
  between operations: 13.9 us -> 0.01 us
  other arithmetic: 10 us -> 0 us
  starting transfers between devices: 8.6 us -> 0 us
  matrix products: 5.98 us -> 0 us
  local copies, waits for them, and re-layouts: 6.09 us -> 3.2 us
    pallas_call x0 -> x1, Pallas kernels: none -> 38.6 us  [body(): pl.pallas_call(functools.partial(kernel, n, nh), out_shape=jax.ShapeDtype...]
    all_gather x1 -> x0, waiting for transfers between devices: 15.3 us -> none  [entering_2(): lax.all_gather(a.astype(kind), axis)]
    ppermute x7 -> x0, waiting for transfers between devices: 12.4 us -> none  [the longest x3 9.79 us: partner(): return lax.ppermute(block, axis, route)]
    all_gather x1 -> x0, blocking collectives: 11.5 us -> none  [entering_2(): lax.all_gather(a.astype(kind), axis)]
    psum x1 -> x0, blocking collectives: 10.2 us -> none  [body(): row_sums = lax.psum(jnp.sum(widened * widened, axis=-1), 'head')]
    ppermute x7 -> x0, starting transfers between devices: 8.6 us -> none  [the longest x3 5.49 us: partner(): return lax.ppermute(block, axis, route)]
    add x11 -> x0, other arithmetic: 7.8 us -> none  [the longest x7 7.78 us: combine_states(): jnp.exp(later[0])[:, None, None] * earlier[1] + later[1]]
    dot_general x9 -> x0, matrix products: 5.98 us -> none  [the longest x1 1.57 us: body(): jnp.einsum('chtu,cuhe->cthe', mixing, inputs_low, preferred_element_type=...]
  transfers between devices with their start and end apart: 8 -> 0, of which waited for: 6 -> 0; matrix products, arithmetic and copies ran while one was open for 6% -> 0% of each run, Pallas kernels for 0% -> 0%
where the time goes in v1:
time: 42 us; the launch traced here: 41.8 us
  Pallas kernels  38.6 us (92%)
  local copies, waits for them, and re-layouts  3.2 us (8%)
    pallas_call x1, Pallas kernels, body(): pl.pallas_call(functools.partial(kernel, n, nh), out_shape=jax.ShapeDtype...  38.6 us
    unnamed x3, local copies, waits for them, and re-layouts  2.52 us

profile of v1, /device:TPU:7, one launch (start us, length us, event | category | flops | bytes accessed | tf_op | source)
XLA Modules:
  0.0 41.8 jit_solution(3074301272650449486)
XLA Ops:
  0.0 0.0 copy-start
  0.0 0.7 %copy-done = f32[16]{0:T(128)S(1)} copy-done((f32[16]{0:T(128)S(1)}, f32[16]{0:T(128)}, u32[]{:S(2)}) %copy-start) | copy-done | bytes 88
  0.7 0.7 %copy.10.skip_ref = f32[16,1]{1,0:T(8,128)} copy(f32[16,1]{0,1:T(1,128)S(1)} %bitcast.3) | data formatting | bytes 128 | tf_op jit(solution)/shard_map/reshape | solution.py:419
  1.3 38.6 %shard_map.91 = bf16[256,1024]{1,0:T(8,128)(2,1)} custom-call(bf16[2,128,1024]{2,1,0:T(8,128)(2,1)} %q_ref.1, bf16[2,128,256]{2,1,0:T(8,128)(2,1)} %k_ref.1, bf16[2,128,256]{2,1,0:T(8,128)(2,1)} %v_ref.1, f32[1,1024]{1,0:T(1,128)} %bitcast.2, bf16[256,128]{1,0:T(8,128)(2,1)} %b_ref.1, bf16[256,128]{1,0:T(8,128)(2,1)} %c_ref.1, f32[16,256]{1,0:T(8,128)} %step_ref.1, ...), custom_call_target="tpu_custom_call" | custom-call | tf_op jit(solution)/shard_map/pallas_call | solution.py:383
  40.0 1.9 %copy.12 = bf16[256,1024]{1,0:T(8,128)(2,1)} copy(bf16[256,1024]{1,0:T(8,128)(2,1)} %shard_map.91) | data formatting | bytes 1048576
Async XLA Ops:
  0.0 0.7 %copy-start = (f32[16]{0:T(128)S(1)}, f32[16]{0:T(128)}, u32[]{:S(2)}) copy-start(f32[16]{0:T(128)} %param.17) | copy-start | bytes 196

commit v2 on v1

--- a/solution.py
+++ b/solution.py
@@ -44,6 +44,7 @@
     tot_buf, tot_own, ms_buf, ms_own, s_own, s_peer, t_chip, s_chips, p_own, p_peer,
     q_send, q_recv, kv_send, kv_recv, fwd_send,
     tot_send, tot_recv, ms_send, ms_recv, a_send, a_recv, b_send, b_recv, c_send, c_recv,
+    rel_k, rel_v, rel_q, rel_send, rel_recv,
 ):
     me = lax.axis_index("seq")
     mz = lax.axis_index("head")
@@ -79,17 +80,52 @@
 
     pl.semaphore_wait(barrier, n + nh - 2)
 
+    quarter = n // 4
+
+    def crosses(s):
+        goal = quarter * s + chip // 2
+        via = 2 * (2 * (goal // 2) + lax.rem(chip, 2)) + core
+        return (lax.rem(goal, 2) != lax.rem(chip, 2)) & (goal // 2 != chip // 2), via
+
+    goal_chip = 2 * (chip // 2) + 1 - lax.rem(chip, 2)
+    relaying = lax.rem(goal_chip, quarter) != chip // 2
+    goal = 2 * goal_chip + lax.rem(chip, 2)
+
+    def relay(g):
+        kcols = pl.ds(g * HDIM, HDIM)
+        qcols = pl.ds(g * gcols, gcols)
+        rows = pl.ds(core * blk, blk)
+        krows = pl.ds((2 + core) * blk, blk)
+        return (
+            (rel_k.at[:, kcols], k_buf.at[krows, kcols], 0, kv_recv.at[g, 2 + core, 0]),
+            (rel_v.at[:, kcols], v_buf.at[krows, kcols], 1, kv_recv.at[g, 2 + core, 1]),
+            (rel_q.at[:, qcols], q_buf.at[rows, qcols], 2, q_recv.at[g, core]),
+        )
+
+    def pass_on(g):
+        @pl.when(relaying)
+        def _():
+            for held, dst, t, rsem in relay(g):
+                arrived(held, rel_recv.at[g, t])
+                remote(held, dst, rel_send.at[g, t], rsem, seq=goal).start()
+
     def moves(g):
         found = []
         for s in range(2):
             home = (n // 2) * s + chip
+            diag, via = crosses(s)
+            straight = jnp.logical_not(diag)
             kcols = pl.ds(g * HDIM, HDIM)
             qcols = pl.ds(g * gcols, gcols)
             for t, (src, dst) in enumerate(((k_ref, k_buf), (v_ref, v_buf))):
                 found.append((
                     src.at[s, :, kcols],
                     dst.at[pl.ds((2 + core) * blk, blk), kcols],
-                    kv_send.at[g, s, 0, t], kv_recv.at[g, 2 + core, t], home, None,
+                    kv_send.at[g, s, 0, t], kv_recv.at[g, 2 + core, t], home, straight,
+                ))
+                found.append((
+                    src.at[s, :, kcols], (rel_k, rel_v)[t].at[:, kcols],
+                    kv_send.at[g, s, 0, t], rel_recv.at[g, t], via, diag,
                 ))
                 found.append((
                     src.at[s, :, kcols],
@@ -100,7 +136,11 @@
             found.append((
                 q_ref.at[s, :, qcols],
                 q_buf.at[pl.ds(core * blk, blk), qcols],
-                q_send.at[g, s], q_recv.at[g, core], home, None,
+                q_send.at[g, s], q_recv.at[g, core], home, straight,
+            ))
+            found.append((
+                q_ref.at[s, :, qcols], rel_q.at[:, qcols],
+                q_send.at[g, s], rel_recv.at[g, 2], via, diag,
             ))
         return found
 
@@ -164,8 +204,7 @@
     cross = dot(c_ref[...], b_ref[...], ((1,), (1,)))
     part[:, 0:toks] = jnp.where(t_ids >= u_ids, cross, 0.0)
 
-    @pl.loop(0, heads)
-    def _(h):
+    def mix_head(h):
         row = cum_buf[pl.ds(h, 1), :]
         col = jnp.transpose(jnp.broadcast_to(row, (LANES, toks)))
         srow = step_ref[pl.ds(h, 1), :]
@@ -173,6 +212,11 @@
             cols = slice(lo, lo + LANES)
             diff = jnp.minimum(col - row[:, cols], 0.0)
             mix[h, :, cols] = (jnp.exp(diff) * part[:, cols] * srow[:, cols]).astype(BF16)
+
+    per = heads // kv_local
+    for g in range(kv_local):
+        pl.loop(g * per, (g + 1) * per)(mix_head)
+        pass_on(g)
 
     factor = math.log2(math.e) / math.sqrt(HDIM)
     r_ids = lax.broadcasted_iota(jnp.int32, (blk, blk), 0)
@@ -299,7 +343,7 @@
         b_copy(dest, chip).start()
 
     left = lax.broadcasted_iota(jnp.int32, (toks, LANES), 1) < sdim
-    skip_row = jnp.sum(skip_ref[...] * pick, axis=0, keepdims=True)
+    skip_row = dot(skip_ref[...], pick, ((1,), (0,)), lax.Precision.HIGHEST)
     for p in range(tiles):
         cols = slice(p * LANES, (p + 1) * LANES)
         x = att[:, cols]
@@ -339,6 +383,11 @@
             @pl.when(away(dest, cond))
             def _():
                 remote(src, dst, ssem, rsem, seq=dest).wait_send()
+
+        @pl.when(relaying)
+        def _():
+            for held, dst, t, rsem in relay(g):
+                remote(held, dst, rel_send.at[g, t], rsem, seq=goal).wait_send()
 
         @pl.when(core == 0)
         def _():
@@ -410,13 +459,17 @@
             dma((kv_local, 2, 2, 2)), dma((kv_local, 4, 2)), dma((kv_local, 2, 2)),
             dma((n,)), dma((n,)), dma((nh,)), dma((nh,)),
             dma, dma, dma((chips,)), dma((chips,)), dma, dma,
+            pltpu.VMEM((blk, kvcols), BF16),
+            pltpu.VMEM((blk, kvcols), BF16),
+            pltpu.VMEM((blk, feats), BF16),
+            dma((kv_local, 3)), dma((kv_local, 3)),
         ],
         compiler_params=pltpu.CompilerParams(
             collective_id=0, has_side_effects=True, vmem_limit_bytes=60 * 2**20
         ),
     )(
         query, keys, values, norm_gain.reshape(1, feats), in_b, out_c, step, log_decay,
-        skip.reshape(heads, 1),
+        skip.reshape(1, heads),
     )
 
 

time: 42 us -> 40 us (0.952)
  local copies, waits for them, and re-layouts: 3.2 us -> 1.87 us
  Pallas kernels: 38.6 us -> 37.9 us
    pallas_call x1, Pallas kernels: 38.6 us -> 37.9 us  [body(): pl.pallas_call(functools.partial(kernel, n, nh), out_shape=jax.ShapeDtype...]
    reshape x1 -> x0, local copies, waits for them, and re-layouts: 0.68 us -> none  [body(): skip.reshape(heads, 1)]
    unnamed x3 -> x1, local copies, waits for them, and re-layouts: 2.52 us -> 1.87 us
where the time goes in v2:
time: 40 us; the launch traced here: 39.8 us
  Pallas kernels  37.9 us (95%)
  local copies, waits for them, and re-layouts  1.87 us (5%)
    pallas_call x1, Pallas kernels, body(): pl.pallas_call(functools.partial(kernel, n, nh), out_shape=jax.ShapeDtype...  37.9 us
    unnamed x1, local copies, waits for them, and re-layouts  1.87 us

profile of v2, /device:TPU:7, one launch (start us, length us, event | category | flops | bytes accessed | tf_op | source)
XLA Modules:
  0.0 39.8 jit_solution(11792164385823258806)
XLA Ops:
  0.0 37.9 %shard_map.91 = bf16[256,1024]{1,0:T(8,128)(2,1)} custom-call(bf16[2,128,1024]{2,1,0:T(8,128)(2,1)} %q_ref.1, bf16[2,128,256]{2,1,0:T(8,128)(2,1)} %k_ref.1, bf16[2,128,256]{2,1,0:T(8,128)(2,1)} %v_ref.1, f32[1,1024]{1,0:T(1,128)} %bitcast.2, bf16[256,128]{1,0:T(8,128)(2,1)} %b_ref.1, bf16[256,128]{1,0:T(8,128)(2,1)} %c_ref.1, f32[16,256]{1,0:T(8,128)} %step_ref.1, ...), custom_call_target="tpu_custom_call" | custom-call | tf_op jit(solution)/shard_map/pallas_call | solution.py:432
  37.9 1.9 %copy.11 = bf16[256,1024]{1,0:T(8,128)(2,1)} copy(bf16[256,1024]{1,0:T(8,128)(2,1)} %shard_map.91) | data formatting | bytes 1048576

commit v3 on v2

--- a/solution.py
+++ b/solution.py
@@ -91,15 +91,19 @@
     relaying = lax.rem(goal_chip, quarter) != chip // 2
     goal = 2 * goal_chip + lax.rem(chip, 2)
 
+    def pieces(g):
+        return [pl.ds(g * gcols + j * HDIM, HDIM) for j in range(group)]
+
     def relay(g):
         kcols = pl.ds(g * HDIM, HDIM)
-        qcols = pl.ds(g * gcols, gcols)
         rows = pl.ds(core * blk, blk)
         krows = pl.ds((2 + core) * blk, blk)
         return (
             (rel_k.at[:, kcols], k_buf.at[krows, kcols], 0, kv_recv.at[g, 2 + core, 0]),
             (rel_v.at[:, kcols], v_buf.at[krows, kcols], 1, kv_recv.at[g, 2 + core, 1]),
-            (rel_q.at[:, qcols], q_buf.at[rows, qcols], 2, q_recv.at[g, core]),
+        ) + tuple(
+            (rel_q.at[:, cols], q_buf.at[rows, cols], 2 + j, q_recv.at[g, core])
+            for j, cols in enumerate(pieces(g))
         )
 
     def pass_on(g):
@@ -136,12 +140,13 @@
             found.append((
                 q_ref.at[s, :, qcols],
                 q_buf.at[pl.ds(core * blk, blk), qcols],
-                q_send.at[g, s], q_recv.at[g, core], home, straight,
+                q_send.at[g, s, 0], q_recv.at[g, core], home, straight,
             ))
-            found.append((
-                q_ref.at[s, :, qcols], rel_q.at[:, qcols],
-                q_send.at[g, s], rel_recv.at[g, 2], via, diag,
-            ))
+            for j, cols in enumerate(pieces(g)):
+                found.append((
+                    q_ref.at[s, :, cols], rel_q.at[:, cols],
+                    q_send.at[g, s, j], rel_recv.at[g, 2 + j], via, diag,
+                ))
         return found
 
     def away(dest, cond):
@@ -216,13 +221,16 @@
     per = heads // kv_local
     for g in range(kv_local):
         pl.loop(g * per, (g + 1) * per)(mix_head)
-        pass_on(g)
+        if g == 0:
+            pass_on(g)
 
     factor = math.log2(math.e) / math.sqrt(HDIM)
     r_ids = lax.broadcasted_iota(jnp.int32, (blk, blk), 0)
     c_ids = lax.broadcasted_iota(jnp.int32, (blk, blk), 1)
     sumsq[...] = jnp.zeros_like(sumsq)
     for g in range(kv_local):
+        if g > 0:
+            pass_on(g)
         kcols = slice(g * HDIM, (g + 1) * HDIM)
         for slot in (2, 3):
             for t, buf in enumerate((k_buf, v_buf)):
@@ -255,7 +263,7 @@
                 q_buf.at[pl.ds(slot * blk, blk), pl.ds(g * gcols, gcols)], q_recv.at[g, slot]
             )
 
-        @pl.loop(0, group)
+        @pl.loop(0, group, unroll=2)
         def _(j):
             hcols = pl.ds(pl.multiple_of(g * gcols + j * HDIM, HDIM), HDIM)
             for slot in (0, 1):
@@ -425,6 +433,7 @@
     heads = step.shape[0]
     nstate = in_b.shape[1]
     tiles = feats // LANES
+    group = tiles // kv_local
     half = feats // 2
     chips = n // 2
     dma = pltpu.SemaphoreType.DMA
@@ -455,14 +464,14 @@
             pltpu.VMEM((chips, nstate, half), BF16),
             pltpu.VMEM((nstate, half), BF16),
             pltpu.VMEM((nstate, half), BF16),
-            dma((kv_local, 2)), dma((kv_local, 2)),
+            dma((kv_local, 2, group)), dma((kv_local, 2)),
             dma((kv_local, 2, 2, 2)), dma((kv_local, 4, 2)), dma((kv_local, 2, 2)),
             dma((n,)), dma((n,)), dma((nh,)), dma((nh,)),
             dma, dma, dma((chips,)), dma((chips,)), dma, dma,
             pltpu.VMEM((blk, kvcols), BF16),
             pltpu.VMEM((blk, kvcols), BF16),
             pltpu.VMEM((blk, feats), BF16),
-            dma((kv_local, 3)), dma((kv_local, 3)),
+            dma((kv_local, 2 + group)), dma((kv_local, 2 + group)),
         ],
         compiler_params=pltpu.CompilerParams(
             collective_id=0, has_side_effects=True, vmem_limit_bytes=60 * 2**20

time: 40 us -> 39.3 us (0.982)
  Pallas kernels: 37.9 us -> 37.1 us
    pallas_call x1, Pallas kernels: 37.9 us -> 37.1 us  [body(): pl.pallas_call(functools.partial(kernel, n, nh), out_shape=jax.ShapeDtype...]
where the time goes in v3:
time: 39.3 us; the launch traced here: 38.9 us
  Pallas kernels  37.1 us (94%)
  local copies, waits for them, and re-layouts  1.87 us (5%)
    pallas_call x1, Pallas kernels, body(): pl.pallas_call(functools.partial(kernel, n, nh), out_shape=jax.ShapeDtype...  37.1 us
    unnamed x1, local copies, waits for them, and re-layouts  1.87 us

profile of v3, /device:TPU:7, one launch (start us, length us, event | category | flops | bytes accessed | tf_op | source)
XLA Modules:
  0.0 38.9 jit_solution(11781141786707314989)
XLA Ops:
  0.0 37.1 %shard_map.91 = bf16[256,1024]{1,0:T(8,128)(2,1)} custom-call(bf16[2,128,1024]{2,1,0:T(8,128)(2,1)} %q_ref.1, bf16[2,128,256]{2,1,0:T(8,128)(2,1)} %k_ref.1, bf16[2,128,256]{2,1,0:T(8,128)(2,1)} %v_ref.1, f32[1,1024]{1,0:T(1,128)} %bitcast.2, bf16[256,128]{1,0:T(8,128)(2,1)} %b_ref.1, bf16[256,128]{1,0:T(8,128)(2,1)} %c_ref.1, f32[16,256]{1,0:T(8,128)} %step_ref.1, ...), custom_call_target="tpu_custom_call" | custom-call | tf_op jit(solution)/shard_map/pallas_call | solution.py:441
  37.1 1.9 %copy.11 = bf16[256,1024]{1,0:T(8,128)(2,1)} copy(bf16[256,1024]{1,0:T(8,128)(2,1)} %shard_map.91) | data formatting | bytes 1048576
